TPU v7x, 256 devices: a whole 4x4x8 slice. The times are simulated.
256 devices in a mesh: rows: 128 (over z, x, y), feat: 2 (over core).
Axes of the slice: x: 4, y: 4, z: 8, core: 2. Of those that a mesh axis runs over, the one named last changes fastest.
Arguments:
- score: float32 [262144, 128], P('rows', 'feat'), may hold values from -4 to 4
- event: int32 [262144, 128], P('rows', 'feat'), may hold values 0 or 1
- leaf: int32 [262144, 128], P('rows', 'feat'), may hold values from 0 to 1
- bins: int32 [262144, 256], P('rows'), may hold values from 0 to 31
- split_feature: int32 [128], P('feat'), may hold values from 0 to 255
- split_bin: int32 [128], P('feat'), may hold values from 0 to 30
Outputs:
- grad_hist: float32 [256, 32, 2, 128], P(('rows', 'feat'))
- hess_hist: float32 [256, 32, 2, 128], P(('rows', 'feat'))
- new_leaf: int32 [262144, 128], P('rows', 'feat')
All inputs are finite; a program needn't handle non-finite values. No bound on the sum of `event` on one device may be relied on, other than what follows from the above.
Results may differ from a plain program's by a relative error of at most 0.0026.
Values may be sent and summed in bfloat16 or wider, within the bound.
No kernel may reach another device: no remote copies, remote signals or barrier semaphores. Data moves between devices by JAX's collectives and lax.ppermute only.
A program may use at most 64 MiB of HBM per device.

v0:
```python
import jax
import jax.numpy as jnp
from jax import lax
from jax.sharding import Mesh
from jax.sharding import PartitionSpec as P

BINS = 32
LEAVES = 2
ROWS = ("rows_0", "rows_1", "rows_2")
ROWS_FEAT = ("rows_0", "rows_1", "rows_2", "feat")


def nothing_yet(x, identity):
    return jax.tree.map(
        lambda a, e: jnp.broadcast_to(jnp.asarray(e, a.dtype), a.shape), x, identity
    )


def carried_in(x, axes, combine, identity):
    before = start = nothing_yet(x, identity)
    so_far = x
    for axis in reversed(axes):
        peers, here = (lax.axis_size(axis), lax.axis_index(axis))
        pieces = lax.all_gather(so_far, axis)
        inside, so_far = (start, start)
        for k in reversed(range(peers)):
            passed = k > here
            so_far = combine(so_far, pieces[k])
            inside = jnp.where(passed, so_far, inside)
        before = combine(inside, before)
    return before


def all_in_one(x, axis):
    leaves = jax.tree.leaves(x)
    order = sorted(range(len(leaves)), key=lambda k: -leaves[k].size)
    width = (1, *leaves[order[0]].shape)[-1]
    lines = [
        jnp.pad(leaves[k].reshape(-1), (0, -leaves[k].size % width)).reshape(-1, width)
        for k in order
    ]
    both, at, found = (lax.all_gather(jnp.concatenate(lines), axis), 0, {})
    for k, line in zip(order, lines):
        section = both[:, at : at + len(line)].reshape(len(both), -1)
        found[k] = section[:, : leaves[k].size].reshape(-1, *leaves[k].shape)
        at += len(line)
    numbers = iter(range(len(leaves)))
    return jax.tree.map(lambda _: found[next(numbers)], x)


def once_a_type(x, axis):
    leaves, found = (jax.tree.leaves(x), {})
    for initial, a in enumerate(leaves):
        if initial not in found:
            alike = [k for k, b in enumerate(leaves) if b.dtype == a.dtype]
            got = (
                all_in_one([leaves[k] for k in alike], axis)
                if len(alike) > 1
                else [lax.all_gather(a, axis)]
            )
            for k, b in zip(alike, got):
                found[k] = b
    numbers = iter(range(len(leaves)))
    return jax.tree.map(lambda _: found[next(numbers)], x)


def prefix_by_axis(x, axes, combine, identity):
    before = start = nothing_yet(x, identity)
    so_far = x
    for axis in reversed(axes):
        peers, here = (lax.axis_size(axis), lax.axis_index(axis))
        pieces = once_a_type(so_far, axis)
        inside, so_far = (start, start)
        for k in range(peers):
            passed = k < here
            so_far = combine(so_far, jax.tree.map(lambda part: part[k], pieces))
            inside = jax.tree.map(lambda new, old: jnp.where(passed, new, old), so_far, inside)
        before = combine(inside, before)
    return before


def copy_for_each(x, axis):
    copies = jnp.broadcast_to(x, (lax.axis_size(axis), *x.shape))
    return lax.all_to_all(copies, axis, split_axis=0, concat_axis=0, tiled=True)


def in_order(tiles, dim):
    dims = list(tiles.shape[1:])
    dims[dim] *= tiles.shape[0]
    return jnp.moveaxis(tiles, 0, dim).reshape(dims)


def collect(x, axis, dim):
    tiles = copy_for_each(x, axis)
    return in_order(tiles, dim)


def in_blocks(x, dim, peers):
    dims = x.shape
    tiles = x.reshape(*dims[:dim], peers, dims[dim] // peers, *dims[dim + 1 :])
    return jnp.moveaxis(tiles, dim, 0)


def scatter_lines(x, axis, dim):
    peers = lax.axis_size(axis)
    tiles = in_blocks(x, dim, peers)
    length = x.size // peers
    spare = max(2048 - length, -length % 1024)
    padded = jnp.pad(tiles.reshape(peers, length), ((0, 0), (0, spare)))
    own = lax.psum_scatter(padded.reshape(-1, 128), axis, scatter_dimension=0, tiled=True)
    return own.reshape(-1)[:length].reshape(tiles.shape[1:])


def combine_sums(earlier_part, later_part):
    return jax.tree.map(jnp.add, earlier_part, later_part)


def histogram(columns, weight_matrix):
    row_count, col_count = columns.shape
    block_rows = min(row_count, 512)
    levels = jnp.arange(BINS, dtype=jnp.int32)

    def hist_step(turn_index, running):
        column_piece = lax.dynamic_slice_in_dim(columns, turn_index * block_rows, block_rows, 0)
        weight_rows = lax.dynamic_slice_in_dim(
            weight_matrix, turn_index * block_rows, block_rows, 0
        )
        onehot = (
            (column_piece[:, :, None] == levels)
            .reshape(block_rows, col_count * BINS)
            .astype(jnp.bfloat16)
        )
        return running + lax.dot_general(
            onehot, weight_rows, (((0,), (0,)), ((), ())), preferred_element_type=jnp.float32
        )

    zeros_init = jnp.zeros((col_count * BINS, weight_matrix.shape[1]), jnp.float32)
    return lax.fori_loop(0, row_count // block_rows, hist_step, zeros_init)


def per_device(score, event, leaf, bins, split_feature, split_bin):
    row_count = score.shape[0]
    shard_count = lax.axis_size(ROWS)
    exp_score = jnp.exp(score)
    event_mass = event.astype(jnp.float32)
    local_suffix = lax.cumsum(exp_score, axis=0, reverse=True)
    risk_total = local_suffix[0]
    later_sum = carried_in(risk_total, ROWS, combine_sums, jnp.zeros_like(risk_total))
    risk_sum = local_suffix + later_sum
    event_share = event_mass / risk_sum
    local_hazard = jnp.cumsum(event_share, axis=0)
    local_square = jnp.cumsum(event_share / risk_sum, axis=0)
    hazard_total = local_hazard[-1]
    square_total = local_square[-1]
    earlier_hazard, earlier_square = prefix_by_axis(
        (hazard_total, square_total),
        ROWS,
        combine_sums,
        (jnp.zeros_like(hazard_total), jnp.zeros_like(square_total)),
    )
    cum_hazard = local_hazard + earlier_hazard
    cum_square = local_square + earlier_square
    scale_factor = BINS * LEAVES / (row_count * shard_count)
    gradient = scale_factor * (exp_score * cum_hazard - event_mass)
    hessian = scale_factor * (exp_score * cum_hazard - exp_score * exp_score * cum_square)
    in_leaf = leaf[:, None, :] == jnp.arange(LEAVES, dtype=jnp.int32)[None, :, None]
    leaf_weights = jnp.stack(
        [
            jnp.where(in_leaf, gradient[:, None, :], jnp.zeros((), jnp.float32)),
            jnp.where(in_leaf, hessian[:, None, :], jnp.zeros((), jnp.float32)),
        ],
        axis=1,
    ).astype(jnp.bfloat16)
    split_value = jnp.take(bins, split_feature, axis=1)
    new_leaf = 2 * leaf + (split_value > split_bin[None, :]).astype(jnp.int32)
    feat_count = lax.axis_size("feat")
    feat_index = lax.axis_index("feat")
    everyone = collect(leaf_weights, "feat", 3)
    weight_matrix = everyone.reshape(row_count, -1)
    per_owner = bins.shape[1] // (shard_count * feat_count)
    grouped = bins.reshape(row_count, shard_count, feat_count, per_owner)
    owned_columns = lax.dynamic_index_in_dim(grouped, feat_index, 2, keepdims=False).reshape(
        row_count, shard_count * per_owner
    )
    summed = scatter_lines(
        histogram(owned_columns, weight_matrix).reshape(
            per_owner * lax.axis_size(ROWS), BINS, 2, LEAVES, -1
        ),
        ROWS,
        0,
    )
    return (summed[:, :, 0], summed[:, :, 1], new_leaf)


def solution(mesh):
    finer = Mesh(
        mesh.devices.reshape(8, 4, 4, mesh.shape["feat"]), ("rows_0", "rows_1", "rows_2", "feat")
    )
    in_specs = (
        P(ROWS, "feat"),
        P(ROWS, "feat"),
        P(ROWS, "feat"),
        P(ROWS, None),
        P("feat"),
        P("feat"),
    )
    out_specs = (P(ROWS_FEAT, None, None, None), P(ROWS_FEAT, None, None, None), P(ROWS, "feat"))
    return jax.shard_map(
        per_device, mesh=finer, in_specs=in_specs, out_specs=out_specs, check_vma=False
    )
```

profile of v0, /device:TPU:0, one launch (start us, length us, event | category | flops | bytes accessed | tf_op | source)
XLA Modules:
  0.0 985.6 jit_solution(2990139637387354905)
XLA Ops:
  8.5 79.3 %reduce-window.20 = f32[64,16,128]{2,1,0:T(8,128)S(1)} reduce-window(f32[64,16,128]{2,1,0:T(8,128)S(1)} %bitcast.142, f32[]{:T(128)} %constant.76.clone.1), window={size=1x1x128 pad=0_0x0_0x0_127}, to_apply=%region_0.0 | reduce-window | flops 16646144 | bytes 1048580 | tf_op jit(solution)/shard_map/reduce-window
  89.0 8.3 all-gather.3
  97.3 9.7 all-gather.4
  107.0 19.1 %all-gather.5 = f32[8,1,64]{2,1,0:T(1,128)S(1)} all-gather(f32[1,1,64]{2,1,0:T(1,128)S(1)} %slice_add_fusion.27), channel_id=1, replica_groups=mesh['rows_0'=8,'rows_1'=4,'rows_2'=4,'feat'=2] {'rows_0'}, dimensions={0}, use_global_device_ids=true | all-gather | bytes 2304 | tf_op jit(solution)/shard_map/all_gather | solution.py:24
  126.6 18.1 %reduce-window.24 = f32[64,16,128]{2,1,0:T(8,128)S(1)} reduce-window(f32[64,16,128]{2,1,0:T(8,128)S(1)} %bitcast.143, f32[]{:T(128)} %constant.76.clone.1), window={size=1x1x128 pad=0_0x0_0x127_0}, to_apply=%region_2.3 | reduce-window | flops 16646144 | bytes 1048580 | tf_op jit(solution)/shard_map/reduce-window.2
  146.2 18.1 %reduce-window.26 = f32[64,16,128]{2,1,0:T(8,128)S(1)} reduce-window(f32[64,16,128]{2,1,0:T(8,128)S(1)} %bitcast.144, f32[]{:T(128)} %constant.76.clone.1), window={size=1x1x128 pad=0_0x0_0x127_0}, to_apply=%region_4.5 | reduce-window | flops 16646144 | bytes 1048580 | tf_op jit(solution)/shard_map/reduce-window.4
  165.8 7.0 all-gather.6
  172.8 7.0 all-gather.7
  179.8 13.3 %all-gather.8 = f32[8,2,64]{2,1,0:T(2,128)S(1)} all-gather(f32[1,2,64]{2,1,0:T(2,128)S(1)} %maximum_bitcast_fusion.2), channel_id=4, replica_groups=mesh['rows_0'=8,'rows_1'=4,'rows_2'=4,'feat'=2] {'rows_0'}, dimensions={0}, use_global_device_ids=true | all-gather | bytes 4608 | tf_op jit(solution)/shard_map/all_gather | solution.py:42
  194.1 1.6 broadcast_in_dim.54
  195.7 4.8 all-to-all-start
  200.8 1.9 copy.45
  202.7 2.2 reshape.569
  205.0 2.7 constant_dynamic-slice_fusion.1
  208.0 3.2 copy.54
  211.2 41.4 %while.14 = (s32[]{:T(128)}, f32[4096,512]{1,0:T(8,128)}, s32[2048,128]{0,1:T(8,128)S(1)}, bf16[2048,512]{0,1:T(8,128)(2,1)}, s32[]{:T(128)}, /*index=5*/s32[]{:T(128)}, s32[]{:T(128)}, s32[]{:T(128)}) while((s32[]{:T(128)}, f32[4096,512]{1,0:T(8,128)}, s32[2048,128]{0,1:T(8,128)S(1)}, bf16[2048,512]{0,1:T(8,128)(2,1)}, s32[]{:T(128)}, ...), condition=%wide.region_7.8_spmd.clone, body=%wide.region_6.7_spmd.clone.sunk | while | flops 2153775104 | bytes 22347932 | solution.py:138
  211.3 1.5 bitcast_compare_fusion.2
  212.8 6.8 select_add_fusion.2
  219.8 1.5 bitcast_compare_fusion.2
  221.3 9.3 select_add_fusion.2
  232.3 9.4 select_add_fusion.2
  243.2 9.3 select_add_fusion.2
  252.6 9.0 reshape.577
  264.3 713.1 %reduce-scatter.2.cloned.1.call-done = f32[128,128]{1,0:T(8,128)} async-done(((f32[16384,128]{1,0:T(8,128)}), f32[128,128]{1,0:T(8,128)}) %reduce-scatter.2.cloned.1.call-update) | async-done | bytes 65552 | tf_op jit(solution)/shard_map/reduce_scatter | solution.py:110
  (75 shorter events, 14.8 us)
Async XLA Ops:
  8.5 117.7 %copy-start = (s32[2048,64]{0,1:T(8,128)S(1)}, s32[2048,64]{0,1:T(8,128)}, u32[]{:S(2)}) copy-start(s32[2048,64]{0,1:T(8,128)} %param.9) | copy-start | bytes 1572868
  164.4 28.8 %copy-start.1 = (f32[2048,64]{0,1:T(8,128)S(1)}, f32[2048,64]{0,1:T(8,128)}, u32[]{:S(2)}) copy-start(f32[2048,64]{0,1:T(8,128)} %param.8) | copy-start | bytes 1572868
  165.4 28.3 %copy-start.2 = (s32[2048,64]{0,1:T(8,128)S(1)}, s32[2048,64]{0,1:T(8,128)}, u32[]{:S(2)}) copy-start(s32[2048,64]{0,1:T(8,128)} %param.10) | copy-start | bytes 1572868
  195.7 12.3 %all-to-all-start = ((bf16[2,2048,2,2,64]{1,4,3,2,0:T(8,128)(2,1)}), bf16[2,2048,2,2,64]{1,4,3,2,0:T(8,128)(2,1)}, u32[]{:S(2)}, u32[]{:S(2)}) async-start(bf16[2,2048,2,2,64]{1,4,3,2,0:T(8,128)(2,1)} %broadcast_in_dim.54), calls=%async_computation | async-start | bytes 4194304 | tf_op jit(solution)/shard_map/all_to_all | solution.py:84
  200.5 776.8 %reduce-scatter.2.cloned.1.call-start = ((), (), s32[]{:S(2)}) async-start(), calls=%async_computation.2 | async-start | bytes 8454144 | tf_op jit(solution)/shard_map/reduce_scatter | solution.py:110
  261.5 0.7 copy-start.5
  262.2 1.0 copy-start.3
  262.2 1.0 copy-start.4
Sparse Core Ops, SparseCore 0:
  261.7 715.6 reduce-scatter.1
where the time goes:
time: 986 us
  waiting for transfers between devices  713 us (72%)
  other arithmetic  125 us (13%)
  blocking collectives  64.4 us (7%)
  matrix products  34.9 us (4%)
  local copies, waits for them, and re-layouts  28.6 us (3%)
  between operations  14.3 us (1%)
    reduce_scatter x1, waiting for transfers between devices, scatter_lines(): lax.psum_scatter(padded.reshape(-1, 128), axis, scatter_dimension=0, tile...  713 us
    another operation x9, other arithmetic  117 us
    all_gather x3, blocking collectives, carried_in(): pieces = lax.all_gather(so_far, axis)  37.1 us
    dot_general x4, matrix products, hist_step(): lax.dot_general(onehot, weight_rows, (((0,), (0,)), ((), ())), preferred_...  34.9 us
    all_gather x3, blocking collectives, all_in_one(): both, at, found = (lax.all_gather(jnp.concatenate(lines), axis), 0, {})  27.3 us
  transfers between devices with their start and end apart: 2, of which 1 were waited for; matrix products, arithmetic and copies ran while one was open for 1% of the time, Pallas kernels for 0%

commit v1 on v0

v1 whole, which is shorter than its diff:
```python
import jax
import jax.numpy as jnp
from jax import lax
from jax.experimental import pallas as pl
from jax.experimental.pallas import tpu as pltpu
from jax.sharding import Mesh
from jax.sharding import PartitionSpec as P

BINS = 32
LEAVES = 2
ROWS = ("rows_0", "rows_1", "rows_2")
PLANE = ("rows_1", "rows_2")
DEPTH_FEAT = ("rows_0", "feat")
ROWS_FEAT = ("rows_0", "rows_1", "rows_2", "feat")
BLOCK = 256
HIGHEST = lax.Precision.HIGHEST
F32 = jnp.float32
DOWN = 2.0**-3


def swap(x, axis):
    return lax.all_to_all(x, axis, split_axis=0, concat_axis=0, tiled=True)


def peers_sum(x, earlier):
    planes = lax.axis_size("rows_0")
    members = lax.axis_size(PLANE)
    here = lax.axis_index(PLANE)
    plane = lax.axis_index("rows_0")
    got = swap(jnp.broadcast_to(x[None], (members, x.shape[0])), PLANE)
    index = lax.broadcasted_iota(jnp.int32, (members, 1), 0)
    chosen = (index < here) if earlier else (index > here)
    inside = jnp.sum(jnp.where(chosen, got, 0.0), axis=0)
    total = jnp.sum(got, axis=0)
    got = swap(jnp.broadcast_to(total[None], (planes, x.shape[0])), "rows_0")
    index = lax.broadcasted_iota(jnp.int32, (planes, 1), 0)
    chosen = (index < plane) if earlier else (index > plane)
    return inside + jnp.sum(jnp.where(chosen, got, 0.0), axis=0)


def as_column(line):
    n = line.shape[1]
    row = lax.broadcasted_iota(jnp.int32, (n, n), 0)
    col = lax.broadcasted_iota(jnp.int32, (n, n), 1)
    return jnp.sum(jnp.where(row == col, jnp.broadcast_to(line, (n, n)), 0.0), axis=1, keepdims=True)


def as_line(column):
    n = column.shape[0]
    row = lax.broadcasted_iota(jnp.int32, (n, n), 0)
    col = lax.broadcasted_iota(jnp.int32, (n, n), 1)
    return jnp.sum(jnp.where(row == col, jnp.broadcast_to(column, (n, n)), 0.0), axis=0, keepdims=True)


def prefix_kernel(score_ref, event_ref, later_ref, local_ref, total_ref):
    width, rows = score_ref.shape
    row = lax.broadcasted_iota(jnp.int32, (BLOCK, BLOCK), 0)
    col = lax.broadcasted_iota(jnp.int32, (BLOCK, BLOCK), 1)
    suffix = (row >= col).astype(F32)
    prefix = (row <= col).astype(F32)
    blocks = rows // BLOCK
    runs = [
        lax.dot(
            jnp.exp(score_ref[:, pl.ds(k * BLOCK, BLOCK)]),
            suffix,
            precision=HIGHEST,
            preferred_element_type=F32,
        )
        for k in range(blocks)
    ]
    carry = as_column(later_ref[...])
    both = [None] * blocks
    for k in reversed(range(blocks)):
        inverse = 1.0 / (runs[k] + carry)
        carry = carry + runs[k][:, :1]
        share = event_ref[:, pl.ds(k * BLOCK, BLOCK)].astype(F32) * inverse
        both[k] = jnp.concatenate([share, share * inverse], axis=0)
    runs = [
        lax.dot(both[k], prefix, precision=HIGHEST, preferred_element_type=F32)
        for k in range(blocks)
    ]
    carry = jnp.zeros((2 * width, 1), F32)
    for k in range(blocks):
        local_ref[:, pl.ds(k * BLOCK, BLOCK)] = runs[k] + carry
        carry = carry + runs[k][:, BLOCK - 1 :]
    total_ref[...] = as_line(carry)


def hist_kernel(score_ref, event_ref, leaf_ref, local_ref, base_ref, bins_ref, out_ref, w_ref):
    width, rows = score_ref.shape
    feats = bins_ref.shape[0]

    @pl.when(pl.program_id(0) == 0)
    def _():
        base = as_column(base_ref[...])
        for k in range(rows // BLOCK):
            at = pl.ds(k * BLOCK, BLOCK)
            e = jnp.exp(score_ref[:, at])
            first = e * (local_ref[:width, at] + base[:width])
            second = e * e * (local_ref[width:, at] + base[width:])
            g = (first - event_ref[:, at].astype(F32)) * DOWN
            h = (first - second) * DOWN
            leaf = leaf_ref[:, at]
            for n, v in enumerate((g, h)):
                for m in range(LEAVES):
                    w_ref[pl.ds((n * LEAVES + m) * width, width), at] = jnp.where(
                        leaf == m, v, 0.0
                    ).astype(jnp.bfloat16)

    group = 8
    level = lax.broadcasted_iota(jnp.int32, (BINS, rows), 0).astype(F32).astype(jnp.bfloat16)
    one = jnp.ones((), jnp.bfloat16)
    zero = jnp.zeros((), jnp.bfloat16)
    for j in range(feats // group):
        tiles = []
        for i in range(group):
            line = bins_ref[pl.ds(j * group + i, 1), :]
            line = jnp.broadcast_to(line, (BINS, rows)).astype(jnp.bfloat16)
            tiles.append(jnp.where(line == level, one, zero))
        hot = jnp.concatenate(tiles, axis=0)
        got = lax.dot_general(
            hot, w_ref[...], (((1,), (1,)), ((), ())), preferred_element_type=F32
        )
        per = out_ref.shape[2]
        n = group * BINS // per
        out_ref[pl.ds(j * n, n), 0] = got.reshape(n, per, got.shape[1])


def per_device(score, event, leaf, bins, split_feature, split_bin):
    rows, width = score.shape
    feats = bins.shape[1]
    shards = lax.axis_size(ROWS)
    planes = lax.axis_size("rows_0")
    members = lax.axis_size(PLANE)
    cores = lax.axis_size("feat")
    cols = 2 * LEAVES * width
    total = jnp.sum(jnp.exp(score), axis=0)
    later = peers_sum(total, False)
    local, sums = pl.pallas_call(
        prefix_kernel,
        out_shape=(
            jax.ShapeDtypeStruct((2 * width, rows), F32),
            jax.ShapeDtypeStruct((1, 2 * width), F32),
        ),
    )(score.T, event.T, later[None])
    base = peers_sum(sums[0], True)
    columns = bins.T.astype(F32)
    slab = feats // planes
    own = BINS * feats // shards
    whole = lambda *shape: pl.BlockSpec(shape, lambda z: (0,) * len(shape))
    parts = pl.pallas_call(
        hist_kernel,
        grid=(planes,),
        in_specs=[
            whole(width, rows),
            whole(width, rows),
            whole(width, rows),
            whole(2 * width, rows),
            whole(1, 2 * width),
            pl.BlockSpec((slab, rows), lambda z: (z, 0)),
        ],
        out_specs=pl.BlockSpec((members, 1, own, cols), lambda z: (0, z, 0, 0)),
        out_shape=jax.ShapeDtypeStruct((members, planes, own, cols), F32),
        scratch_shapes=[pltpu.VMEM((cols, rows), jnp.bfloat16)],
    )(score.T, event.T, leaf.T, local, base[None], columns)
    got = swap(parts.astype(jnp.float16), PLANE)
    plane_sum = jnp.sum(got.astype(F32), axis=0)
    got = swap(plane_sum.reshape(planes * cores, own // cores, cols), DEPTH_FEAT)
    summed = jnp.sum(got.reshape(planes, cores, own // cores, cols), axis=0)
    summed = summed * (BINS * LEAVES / (rows * shards) / DOWN)
    summed = summed.reshape(cores, BINS, 2, LEAVES, width)
    summed = jnp.moveaxis(summed, 0, 3).reshape(1, BINS, 2, LEAVES, cores * width)
    split_value = jnp.take(bins, split_feature, axis=1)
    new_leaf = 2 * leaf + (split_value > split_bin[None, :]).astype(jnp.int32)
    return (summed[:, :, 0], summed[:, :, 1], new_leaf)


def solution(mesh):
    finer = Mesh(
        mesh.devices.reshape(8, 4, 4, mesh.shape["feat"]), ("rows_0", "rows_1", "rows_2", "feat")
    )
    in_specs = (
        P(ROWS, "feat"),
        P(ROWS, "feat"),
        P(ROWS, "feat"),
        P(ROWS, None),
        P("feat"),
        P("feat"),
    )
    out_specs = (P(ROWS_FEAT, None, None, None), P(ROWS_FEAT, None, None, None), P(ROWS, "feat"))
    return jax.shard_map(
        per_device, mesh=finer, in_specs=in_specs, out_specs=out_specs, check_vma=False
    )
```

time: 986 us -> 158 us (0.16)
  the two profiles are of different devices: /device:TPU:0 before, /device:TPU:1 now
where the time goes in v1:
time: 158 us
  blocking collectives  46.9 us (30%)
  waiting for transfers between devices  37.1 us (23%)
  starting transfers between devices  34.4 us (22%)
  Pallas kernels  18.3 us (12%)
  other arithmetic  12.4 us (8%)
  local copies, waits for them, and re-layouts  7.66 us (5%)
    all_to_all x1, blocking collectives, swap(): return lax.all_to_all(x, axis, split_axis=0, concat_axis=0, tiled=True)  46.9 us
    all_to_all x5, waiting for transfers between devices, swap(): return lax.all_to_all(x, axis, split_axis=0, concat_axis=0, tiled=True)  37.1 us
    all_to_all x5, starting transfers between devices, swap(): return lax.all_to_all(x, axis, split_axis=0, concat_axis=0, tiled=True)  34.4 us
    pallas_call x1, Pallas kernels, per_device(): pl.pallas_call(hist_kernel, grid=(planes,), in_specs=[whole(width, rows),...  13.8 us
    pallas_call x1, Pallas kernels, per_device(): pl.pallas_call(prefix_kernel, out_shape=(jax.ShapeDtypeStruct((2 * width,...  4.55 us
    convert_element_type x1, other arithmetic, per_device(): got = swap(parts.astype(jnp.float16), PLANE)  4.19 us
    unnamed x9, local copies, waits for them, and re-layouts  3.47 us
  transfers between devices with their start and end apart: 5, of which 5 were waited for; matrix products, arithmetic and copies ran while one was open for 4% of the time, Pallas kernels for 0%

profile of v1, /device:TPU:1, one launch (start us, length us, event | category | flops | bytes accessed | tf_op | source)
XLA Modules:
  0.0 157.6 jit_solution(12280779724303691622)
XLA Ops:
  0.6 1.2 exponential_reduce_fusion
  2.5 7.6 %all-to-all-start = ((f32[16,1,64]{2,1,0:T(1,128)}), f32[16,1,64]{2,1,0:T(1,128)S(1)}, u32[]{:S(2)}, u32[]{:S(2)}) async-start(f32[16,1,64]{2,1,0:T(1,128)} %broadcast_in_dim.87), calls=%async_computation | async-start | bytes 16384 | tf_op jit(solution)/shard_map/all_to_all | solution.py:22
  10.1 1.9 %copy.23 = s32[2048,256]{0,1:T(8,128)S(1)} copy(s32[2048,256]{1,0:T(8,128)} %param.9) | data formatting | bytes 4194304 | tf_op args[3]
  12.0 1.6 %convert_bitcast_fusion.bins_ref = f32[256,2048]{1,0:T(8,128)} fusion(s32[2048,256]{0,1:T(8,128)S(1)} %copy.23), kind=kLoop, calls=%fused_computation.2 | loop fusion | flops 524288 | bytes 4194304 | tf_op jit(solution)/shard_map/convert_element_type | solution.py:147
  13.7 2.8 %all-to-all-done = f32[16,1,64]{2,1,0:T(1,128)S(1)} async-done(((f32[16,1,64]{2,1,0:T(1,128)}), f32[16,1,64]{2,1,0:T(1,128)S(1)}, u32[]{:S(2)}, u32[]{:S(2)}) %all-to-all-start) | async-done | bytes 4128 | tf_op jit(solution)/shard_map/all_to_all | solution.py:22
  17.0 8.2 %all-to-all-start.1 = ((f32[8,1,64]{2,1,0:T(1,128)}), f32[8,1,64]{2,1,0:T(1,128)S(1)}, u32[]{:S(2)}, u32[]{:S(2)}) async-start(f32[8,1,64]{2,1,0:T(1,128)} %broadcast_in_dim.90), calls=%async_computation.1 | async-start | bytes 8192 | tf_op jit(solution)/shard_map/all_to_all | solution.py:22
  25.3 6.4 %all-to-all-done.1 = f32[8,1,64]{2,1,0:T(1,128)S(1)} async-done(((f32[8,1,64]{2,1,0:T(1,128)}), f32[8,1,64]{2,1,0:T(1,128)S(1)}, u32[]{:S(2)}, u32[]{:S(2)}) %all-to-all-start.1) | async-done | bytes 2080 | tf_op jit(solution)/shard_map/all_to_all | solution.py:22
  32.3 4.5 %shard_map.85 = (f32[128,2048]{1,0:T(8,128)}, f32[1,128]{1,0:T(1,128)}) custom-call(f32[64,2048]{1,0:T(8,128)} %bitcast.25, s32[64,2048]{1,0:T(8,128)} %bitcast.27, f32[1,64]{1,0:T(1,128)} %add_bitcast_fusion.1.later_ref), custom_call_target="tpu_custom_call" | custom-call | tf_op jit(solution)/shard_map/pallas_call | solution.py:139
  36.9 1.3 broadcast_in_dim.93
  38.1 3.9 %all-to-all-start.2 = ((f32[16,1,128]{2,1,0:T(1,128)}), f32[16,1,128]{2,1,0:T(1,128)S(1)}, u32[]{:S(2)}, u32[]{:S(2)}) async-start(f32[16,1,128]{2,1,0:T(1,128)} %broadcast_in_dim.93), calls=%async_computation.2 | async-start | bytes 16384 | tf_op jit(solution)/shard_map/all_to_all | solution.py:22
  42.0 6.4 %all-to-all-done.2 = f32[16,1,128]{2,1,0:T(1,128)S(1)} async-done(((f32[16,1,128]{2,1,0:T(1,128)}), f32[16,1,128]{2,1,0:T(1,128)S(1)}, u32[]{:S(2)}, u32[]{:S(2)}) %all-to-all-start.2) | async-done | bytes 8224 | tf_op jit(solution)/shard_map/all_to_all | solution.py:22
  49.0 3.3 %all-to-all-start.3 = ((f32[8,1,128]{2,1,0:T(1,128)}), f32[8,1,128]{2,1,0:T(1,128)S(1)}, u32[]{:S(2)}, u32[]{:S(2)}) async-start(f32[8,1,128]{2,1,0:T(1,128)} %broadcast_in_dim.96), calls=%async_computation.3 | async-start | bytes 8192 | tf_op jit(solution)/shard_map/all_to_all | solution.py:22
  52.4 6.3 %all-to-all-done.3 = f32[8,1,128]{2,1,0:T(1,128)S(1)} async-done(((f32[8,1,128]{2,1,0:T(1,128)}), f32[8,1,128]{2,1,0:T(1,128)S(1)}, u32[]{:S(2)}, u32[]{:S(2)}) %all-to-all-start.3) | async-done | bytes 4128 | tf_op jit(solution)/shard_map/all_to_all | solution.py:22
  59.3 13.8 %shard_map.86 = f32[16,8,64,256]{3,2,1,0:T(8,128)} custom-call(f32[64,2048]{1,0:T(8,128)} %bitcast.26, s32[64,2048]{1,0:T(8,128)} %bitcast.28, s32[64,2048]{1,0:T(8,128)} %bitcast.29, f32[128,2048]{1,0:T(8,128)} %get-tuple-element.5.local_ref, f32[1,128]{1,0:T(1,128)} %add_bitcast_fusion.base_ref, f32[256,2048]{1,0:T(8,128)} %convert_bitcast_fusion.bins_ref), custom_call_target="tpu_custom_call" | custom-call | tf_op jit(solution)/shard_map/pallas_call | solution.py:151
  73.1 4.2 %convert_element_type.16 = f16[16,8,64,256]{3,2,1,0:T(8,128)(2,1)S(1)} convert(f32[16,8,64,256]{3,2,1,0:T(8,128)} %shard_map.86) | non-fusion elementwise | flops 2097152 | bytes 12582912 | tf_op jit(solution)/shard_map/convert_element_type | solution.py:166
  77.3 46.9 %all_to_all.46 = f16[16,8,64,256]{3,2,1,0:T(8,128)(2,1)S(1)} all-to-all(f16[16,8,64,256]{3,2,1,0:T(8,128)(2,1)S(1)} %convert_element_type.16), channel_id=1, replica_groups=mesh['rows_0'=8,'rows_1'=4,'rows_2'=4,'feat'=2] {'rows_1','rows_2'}, dimensions={0} | all-to-all | bytes 8388608 | tf_op jit(solution)/shard_map/all_to_all | solution.py:22
  124.2 1.7 %convert_reduce_fusion = f32[8,64,256]{2,1,0:T(8,128)} fusion(f16[16,8,64,256]{3,2,1,0:T(8,128)(2,1)S(1)} %all_to_all.46), kind=kLoop, calls=%fused_computation.1 | loop fusion | flops 4063232 | bytes 4718592 | tf_op jit(solution)/shard_map/reduce_sum | solution.py:167
  126.0 11.5 %all-to-all-start.5 = ((f32[16,32,256]{2,1,0:T(8,128)}), f32[16,32,256]{2,1,0:T(8,128)}, u32[]{:S(2)}, u32[]{:S(2)}) async-start(f32[16,32,256]{2,1,0:T(8,128)} %bitcast.11), calls=%async_computation.5 | async-start | bytes 1048576 | tf_op jit(solution)/shard_map/all_to_all | solution.py:22
  137.5 0.8 gather_fusion
  138.5 1.0 bitcast_add_fusion
  139.6 15.3 %all-to-all-done.5 = f32[16,32,256]{2,1,0:T(8,128)} async-done(((f32[16,32,256]{2,1,0:T(8,128)}), f32[16,32,256]{2,1,0:T(8,128)}, u32[]{:S(2)}, u32[]{:S(2)}) %all-to-all-start.5) | async-done | bytes 524320 | tf_op jit(solution)/shard_map/all_to_all | solution.py:22
  154.9 1.1 reduce_sum.89
  156.3 0.6 copy.27
  157.0 0.6 copy.26
  (29 shorter events, 3.9 us)
Async XLA Ops:
  2.5 13.9 %all-to-all-start = ((f32[16,1,64]{2,1,0:T(1,128)}), f32[16,1,64]{2,1,0:T(1,128)S(1)}, u32[]{:S(2)}, u32[]{:S(2)}) async-start(f32[16,1,64]{2,1,0:T(1,128)} %broadcast_in_dim.87), calls=%async_computation | async-start | bytes 16384 | tf_op jit(solution)/shard_map/all_to_all | solution.py:22
  17.0 14.7 %all-to-all-start.1 = ((f32[8,1,64]{2,1,0:T(1,128)}), f32[8,1,64]{2,1,0:T(1,128)S(1)}, u32[]{:S(2)}, u32[]{:S(2)}) async-start(f32[8,1,64]{2,1,0:T(1,128)} %broadcast_in_dim.90), calls=%async_computation.1 | async-start | bytes 8192 | tf_op jit(solution)/shard_map/all_to_all | solution.py:22
  38.1 10.3 %all-to-all-start.2 = ((f32[16,1,128]{2,1,0:T(1,128)}), f32[16,1,128]{2,1,0:T(1,128)S(1)}, u32[]{:S(2)}, u32[]{:S(2)}) async-start(f32[16,1,128]{2,1,0:T(1,128)} %broadcast_in_dim.93), calls=%async_computation.2 | async-start | bytes 16384 | tf_op jit(solution)/shard_map/all_to_all | solution.py:22
  49.0 9.7 %all-to-all-start.3 = ((f32[8,1,128]{2,1,0:T(1,128)}), f32[8,1,128]{2,1,0:T(1,128)S(1)}, u32[]{:S(2)}, u32[]{:S(2)}) async-start(f32[8,1,128]{2,1,0:T(1,128)} %broadcast_in_dim.96), calls=%async_computation.3 | async-start | bytes 8192 | tf_op jit(solution)/shard_map/all_to_all | solution.py:22
  124.2 13.2 %copy-start.2 = (s32[64]{0:T(128)S(1)}, s32[64]{0:T(128)}, u32[]{:S(2)}) copy-start(s32[64]{0:T(128)} %param.10) | copy-start | bytes 772
  126.0 28.9 %all-to-all-start.5 = ((f32[16,32,256]{2,1,0:T(8,128)}), f32[16,32,256]{2,1,0:T(8,128)}, u32[]{:S(2)}, u32[]{:S(2)}) async-start(f32[16,32,256]{2,1,0:T(8,128)} %bitcast.11), calls=%async_computation.5 | async-start | bytes 1048576 | tf_op jit(solution)/shard_map/all_to_all | solution.py:22
  137.5 1.0 copy-start
  137.5 1.0 copy-start.1

commit v2 on v1

v2 whole, which is shorter than its diff:
```python
import jax
import jax.numpy as jnp
from jax import lax
from jax.experimental import pallas as pl
from jax.experimental.pallas import tpu as pltpu
from jax.sharding import Mesh
from jax.sharding import PartitionSpec as P

BINS = 32
LEAVES = 2
AXES = ("far", "mate", "across", "down", "feat")
ROWS = AXES[:4]
PLANE = ("across", "down")
BLOCK = 256
F32 = jnp.float32
VMEM = 28 << 20
DOWN = 2.0**-3


def swap(x, axis):
    return lax.all_to_all(x, axis, split_axis=0, concat_axis=0, tiled=True)


def chosen_sum(got, here, earlier):
    index = lax.broadcasted_iota(jnp.int32, got.shape, 0)
    chosen = (index < here) if earlier else (index > here)
    return jnp.sum(jnp.where(chosen, got, 0.0), axis=0, keepdims=True)


def as_column(line):
    n = line.shape[1]
    row = lax.broadcasted_iota(jnp.int32, (n, n), 0)
    col = lax.broadcasted_iota(jnp.int32, (n, n), 1)
    return jnp.sum(jnp.where(row == col, jnp.broadcast_to(line, (n, n)), 0.0), axis=1, keepdims=True)


def as_line(column):
    n = column.shape[0]
    row = lax.broadcasted_iota(jnp.int32, (n, n), 0)
    col = lax.broadcasted_iota(jnp.int32, (n, n), 1)
    return jnp.sum(jnp.where(row == col, jnp.broadcast_to(column, (n, n)), 0.0), axis=0, keepdims=True)


def split_dot(x, ones):
    high = x.astype(jnp.bfloat16)
    rest = x - high.astype(F32)
    middle = rest.astype(jnp.bfloat16)
    low = (rest - middle.astype(F32)).astype(jnp.bfloat16)
    dot = lambda part: lax.dot(part, ones, preferred_element_type=F32)
    return (dot(low) + dot(middle)) + dot(high)


def total_kernel(score_ref, total_ref):
    total = jnp.sum(jnp.exp(score_ref[...]), axis=1, keepdims=True)
    total_ref[...] = jnp.broadcast_to(as_line(total), total_ref.shape)


def prefix_kernel(here_ref, score_ref, event_ref, later_ref, local_ref, total_ref):
    width, rows = score_ref.shape
    row = lax.broadcasted_iota(jnp.int32, (BLOCK, BLOCK), 0)
    col = lax.broadcasted_iota(jnp.int32, (BLOCK, BLOCK), 1)
    suffix = (row >= col).astype(F32).astype(jnp.bfloat16)
    prefix = (row <= col).astype(F32).astype(jnp.bfloat16)
    blocks = rows // BLOCK
    at = lambda k: pl.ds(k * BLOCK, BLOCK)
    e = jnp.concatenate([jnp.exp(score_ref[:, at(k)]) for k in range(blocks)], axis=0)
    runs = split_dot(e, suffix)
    carry = as_column(chosen_sum(later_ref[...], here_ref[0], False))
    both = [None] * blocks
    for k in reversed(range(blocks)):
        run = runs[k * width : (k + 1) * width]
        inverse = 1.0 / (run + carry)
        carry = carry + run[:, :1]
        share = event_ref[:, at(k)].astype(F32) * inverse
        both[k] = jnp.concatenate([share, share * inverse], axis=0)
    runs = split_dot(jnp.concatenate(both, axis=0), prefix)
    carry = jnp.zeros((2 * width, 1), F32)
    for k in range(blocks):
        run = runs[2 * k * width : 2 * (k + 1) * width]
        local_ref[:, at(k)] = run + carry
        carry = carry + run[:, BLOCK - 1 :]
    total_ref[...] = jnp.broadcast_to(as_line(carry), total_ref.shape)


def weigh_kernel(here_ref, base_ref, *refs):
    w_ref = refs[-1]
    for part in range(2):
        score_ref, event_ref, leaf_ref, local_ref = refs[4 * part : 4 * part + 4]
        width, rows = score_ref.shape
        base = as_column(chosen_sum(base_ref[...], here_ref[part], True))
        for k in range(rows // BLOCK):
            at = pl.ds(k * BLOCK, BLOCK)
            e = jnp.exp(score_ref[:, at])
            first = e * (local_ref[:width, at] + base[:width])
            second = e * e * (local_ref[width:, at] + base[width:])
            g = (first - event_ref[:, at].astype(F32)) * DOWN
            h = (first - second) * DOWN
            leaf = leaf_ref[:, at].astype(F32)
            for n, v in enumerate((g, h)):
                for m in range(LEAVES):
                    w_ref[
                        pl.ds((n * LEAVES + m) * width, width), pl.ds(part * rows + k * BLOCK, BLOCK)
                    ] = jnp.where(leaf == float(m), v, 0.0).astype(jnp.bfloat16)


def hist_kernel(w_ref, own_ref, mate_ref, out_ref):
    feats, rows = own_ref.shape
    level = lax.broadcasted_iota(jnp.int32, (BINS, 2 * rows), 0).astype(F32).astype(jnp.bfloat16)
    one = jnp.ones((), jnp.bfloat16)
    zero = jnp.zeros((), jnp.bfloat16)
    tiles = []
    for i in range(feats):
        line = jnp.concatenate([own_ref[pl.ds(i, 1), :], mate_ref[pl.ds(i, 1), :]], axis=1)
        line = jnp.broadcast_to(line, (BINS, 2 * rows)).astype(jnp.bfloat16)
        tiles.append(jnp.where(line == level, one, zero))
    hot = jnp.concatenate(tiles, axis=0)
    got = lax.dot_general(hot, w_ref[...], (((1,), (1,)), ((), ())), preferred_element_type=F32)
    out_ref[:, 0] = got.reshape(out_ref.shape[0], *out_ref.shape[2:])


def per_device(score, event, leaf, bins, split_feature, split_bin):
    rows, width = score.shape
    feats = bins.shape[1]
    shards = lax.axis_size(ROWS)
    cores = lax.axis_size("feat")
    cols = 2 * LEAVES * width
    far, mate, across, down = (lax.axis_size(a) for a in ROWS)
    members = across * down
    here = lax.axis_index(ROWS).astype(jnp.int32)
    both = jnp.stack([here, here ^ members])
    turned = both[::-1]
    scalar = pl.BlockSpec(memory_space=pltpu.SMEM)
    dense = pl.BlockSpec(memory_space=pltpu.VMEM)
    limit = pltpu.CompilerParams(vmem_limit_bytes=VMEM)
    pair = [(0, 1), (1, 0)]
    send = lambda x: lax.ppermute(x, "mate", pair)
    mate_score = send(score.T)
    copies = pl.pallas_call(
        total_kernel,
        out_shape=jax.ShapeDtypeStruct((shards, width), F32),
        compiler_params=limit,
    )(score.T)
    copies, score, event, leaf, bins = lax.optimization_barrier((copies, score, event, leaf, bins))
    totals = swap(copies, ROWS)
    columns = bins.T.astype(jnp.bfloat16).reshape(far, mate, -1, rows)
    side = lax.axis_index("mate")
    pick = lambda k: lax.dynamic_index_in_dim(columns, k, 1, keepdims=False).reshape(-1, rows)
    own_columns = pick(side).astype(F32)
    mate_event = send(event.T.astype(jnp.bfloat16))
    mate_columns = send(pick(1 - side))
    mate_leaf = send(leaf.T.astype(jnp.bfloat16))

    prefix = lambda order, s, e: pl.pallas_call(
        prefix_kernel,
        in_specs=[scalar, dense, dense, dense],
        out_shape=(
            jax.ShapeDtypeStruct((2 * width, rows), F32),
            jax.ShapeDtypeStruct((shards, 2 * width), F32),
        ),
        compiler_params=limit,
    )(order, s, e, totals)
    local, copies = prefix(both, score.T, event.T)
    base = swap(copies, ROWS)
    mate_local, _ = prefix(turned, mate_score, mate_event)
    weights = pl.pallas_call(
        weigh_kernel,
        in_specs=[scalar] + [dense] * 9,
        out_shape=jax.ShapeDtypeStruct((cols, 2 * rows), jnp.bfloat16),
        compiler_params=limit,
    )(both, base, score.T, event.T, leaf.T, local, mate_score, mate_event, mate_leaf, mate_local)
    own = cores * BINS
    step = members // 2
    slab = step * cores
    columns = pl.BlockSpec((slab, rows), lambda z, j: (2 * z + j, 0))
    parts = pl.pallas_call(
        hist_kernel,
        grid=(far, 2),
        in_specs=[pl.BlockSpec((cols, 2 * rows), lambda z, j: (0, 0)), columns, columns],
        out_specs=pl.BlockSpec((step, 1, own, cols), lambda z, j: (j, z, 0, 0)),
        out_shape=jax.ShapeDtypeStruct((members, far, own, cols), F32),
        compiler_params=limit,
    )(weights, own_columns, mate_columns.astype(F32))
    got = jnp.sum(swap(parts.astype(jnp.float16), PLANE).astype(F32), axis=0)
    got = swap(got.reshape(far * cores, BINS, cols), ("far", "feat"))
    summed = jnp.sum(got.reshape(far, cores, BINS, cols), axis=0)
    summed = summed * (BINS * LEAVES / (rows * shards) / DOWN)
    summed = summed.reshape(cores, BINS, 2, LEAVES, width)
    summed = jnp.moveaxis(summed, 0, 3).reshape(1, BINS, 2, LEAVES, cores * width)
    split_value = jnp.take(bins, split_feature, axis=1)
    new_leaf = 2 * leaf + (split_value > split_bin[None, :]).astype(jnp.int32)
    return (summed[:, :, 0], summed[:, :, 1], new_leaf)


def solution(mesh):
    finer = Mesh(
        mesh.devices.reshape(4, 2, 4, 4, mesh.shape["feat"]), AXES
    )
    in_specs = (
        P(ROWS, "feat"),
        P(ROWS, "feat"),
        P(ROWS, "feat"),
        P(ROWS, None),
        P("feat"),
        P("feat"),
    )
    out_specs = (P(AXES, None, None, None), P(AXES, None, None, None), P(ROWS, "feat"))
    return jax.shard_map(
        per_device, mesh=finer, in_specs=in_specs, out_specs=out_specs, check_vma=False
    )
```

time: 158 us -> 125 us (0.79)
  waiting for transfers between devices: 37.1 us -> 5.08 us
  other arithmetic: 12.4 us -> 7.47 us
  local copies, waits for them, and re-layouts: 7.66 us -> 12.5 us
  starting transfers between devices: 34.4 us -> 32.5 us
    all_to_all x5 -> x2, waiting for transfers between devices: 37.1 us -> 5.07 us  [swap(): return lax.all_to_all(x, axis, split_axis=0, concat_axis=0, tiled=True)]
    all_to_all x5 -> x2, starting transfers between devices: 34.4 us -> 27.8 us  [swap(): return lax.all_to_all(x, axis, split_axis=0, concat_axis=0, tiled=True)]
    ppermute x0 -> x4, starting transfers between devices: none -> 4.68 us  [per_device(): send = lambda x: lax.ppermute(x, 'mate', pair)]
    unnamed x9 -> x22, local copies, waits for them, and re-layouts: 3.47 us -> 8.11 us
    reduce_sum x9 -> x2, other arithmetic: 4.44 us -> 0.4 us  [the longest x1 0.39 us: per_device(): got = jnp.sum(swap(parts.astype(jnp.float16), PLANE).astype(F32), axis=0)]
    broadcast_in_dim x4 -> x0, local copies, waits for them, and re-layouts: 3.07 us -> none  [the longest x2 1.87 us: peers_sum(): got = swap(jnp.broadcast_to(x[None], (members, x.shape[0])), PLANE)]
    optimization_barrier x0 -> x1, local copies, waits for them, and re-layouts: none -> 1.92 us  [per_device(): lax.optimization_barrier((copies, score, event, leaf, bins))]
    convert_element_type x2 -> x5, other arithmetic: 5.81 us -> 4.62 us  [the longest x1 1.77 us: per_device(): mate_event = send(event.T.astype(jnp.bfloat16))]
  transfers between devices with their start and end apart: 5 -> 6, of which waited for: 5 -> 1; matrix products, arithmetic and copies ran while one was open for 4% -> 9% of each run, Pallas kernels for 0% -> 5%
where the time goes in v2:
time: 125 us; the launch traced here: 124 us
  blocking collectives  46.8 us (37%)
  starting transfers between devices  32.5 us (26%)
  Pallas kernels  19.3 us (15%)
  local copies, waits for them, and re-layouts  12.5 us (10%)
  other arithmetic  7.47 us (6%)
  waiting for transfers between devices  5.08 us (4%)
    all_to_all x2, blocking collectives, swap(): return lax.all_to_all(x, axis, split_axis=0, concat_axis=0, tiled=True)  46.8 us
    all_to_all x2, starting transfers between devices, swap(): return lax.all_to_all(x, axis, split_axis=0, concat_axis=0, tiled=True)  27.8 us
    pallas_call x1, Pallas kernels, per_device(): pl.pallas_call(hist_kernel, grid=(far, 2), in_specs=[pl.BlockSpec((cols,...  10.5 us
    unnamed x22, local copies, waits for them, and re-layouts  8.11 us
    pallas_call x2, Pallas kernels, per_device(): pl.pallas_call(prefix_kernel, in_specs=[scalar, dense, dense, dense], out...  5.77 us
    all_to_all x2, waiting for transfers between devices, swap(): return lax.all_to_all(x, axis, split_axis=0, concat_axis=0, tiled=True)  5.07 us
    ppermute x4, starting transfers between devices, per_device(): send = lambda x: lax.ppermute(x, 'mate', pair)  4.68 us
  transfers between devices with their start and end apart: 6, of which 1 were waited for; matrix products, arithmetic and copies ran while one was open for 9% of the time, Pallas kernels for 5%

profile of v2, /device:TPU:1, one launch (start us, length us, event | category | flops | bytes accessed | tf_op | source)
XLA Modules:
  0.0 124.4 jit_solution(3098221490817346911)
XLA Ops:
  0.6 2.5 %collective-permute-start = (f32[64,2048]{1,0:T(8,128)}, f32[64,2048]{1,0:T(8,128)}, u32[]{:S(2)}, u32[]{:S(2)}) collective-permute-start(f32[64,2048]{1,0:T(8,128)} %bitcast.34), channel_id=1, source_target_pairs={{0,32},{32,0},{1,33},{33,1},{2,34},{34,2},{3,35},{35,3},{4,36},{36... | collective-permute-start | bytes 1572872 | tf_op jit(solution)/shard_map/ppermute | solution.py:136
  3.2 1.1 copy-done
  4.2 0.8 shard_map.85
  5.0 14.6 %all-to-all-start = ((f32[128,1,64]{2,1,0:T(1,128)}), f32[128,1,64]{2,1,0:T(1,128)S(1)}, u32[]{:S(2)}, u32[]{:S(2)}) async-start(f32[128,1,64]{2,1,0:T(1,128)} %bitcast.6), calls=%async_computation | async-start | bytes 131072 | tf_op jit(solution)/shard_map/all_to_all | solution.py:21
  19.7 1.8 %bitcast_convert_fusion.2 = bf16[64,2048]{1,0:T(8,128)(2,1)} fusion(s32[2048,64]{0,1:T(8,128)} %param.7), kind=kLoop, calls=%fused_computation.15 | loop fusion | flops 131072 | bytes 786432 | tf_op jit(solution)/shard_map/convert_element_type | solution.py:149
  23.3 1.9 %copy.28 = s32[2048,256]{0,1:T(8,128)S(1)} copy(s32[2048,256]{1,0:T(8,128)} %param.9) | data formatting | bytes 4194304 | tf_op jit(solution)/shard_map/optimization_barrier | solution.py:143
  26.3 1.0 bitcast_add_fusion
  27.3 0.9 collective-permute-start.2
  28.2 1.1 convert_element_type.31
  29.4 1.3 %constant_dynamic-slice_fusion = (bf16[4,1,32,2048]{3,2,1,0:T(8,128)(2,1)S(1)}, bf16[4,1,32,2048]{3,2,1,0:T(8,128)(2,1)S(1)}) fusion(bf16[4,2,32,2048]{3,2,1,0:T(8,128)(2,1)} %bitcast.44, s32[]{:T(128)S(6)} %select_n.17, s32[]{:T(128)S(6)} %select_n.16), kind=kLoop, calls=%fused_computation.12 | loop fusion | bytes 2097160 | tf_op jit(solution)/shard_map/jit(dynamic_index_in_dim)/dynamic_slice | solution.py:147
  31.4 2.6 %shard_map.86 = (f32[128,2048]{1,0:T(8,128)S(1)}, f32[128,128]{1,0:T(8,128)}) custom-call(s32[2]{0:T(128)S(1)} %pad_add_fusion.here_ref, f32[64,2048]{1,0:T(8,128)S(1)} %bitcast.36, s32[64,2048]{1,0:T(8,128)S(1)} %bitcast.38, f32[128,64]{1,0:T(8,128)S(1)} %bitcast.41), custom_call_target="tpu_custom_call" | custom-call | tf_op jit(solution)/shard_map/pallas_call | solution.py:153
  34.1 1.0 copy-done.5
  35.0 13.2 %all-to-all-start.1 = ((f32[128,1,128]{2,1,0:T(1,128)}), f32[128,1,128]{2,1,0:T(1,128)S(1)}, u32[]{:S(2)}, u32[]{:S(2)}) async-start(f32[128,1,128]{2,1,0:T(1,128)} %bitcast.9), calls=%async_computation.1 | async-start | bytes 131072 | tf_op jit(solution)/shard_map/all_to_all | solution.py:21
  48.5 1.1 convert_element_type.35.mate_ref
  49.6 3.1 %shard_map.87 = (f32[128,2048]{1,0:T(8,128)S(1)}, f32[128,128]{1,0:T(8,128)}) custom-call(s32[2]{0:T(128)S(1)} %rev.3.here_ref, f32[64,2048]{1,0:T(8,128)} %collective-permute-done.score_ref.refs_4_, bf16[64,2048]{1,0:T(8,128)(2,1)S(1)} %collective-permute-done.1.event_ref.refs_5_, f32[128,64]{1,0:T(8,128)S(1)} %bitcast.42), custom_call_target="tpu_custom_call" | custom-call | tf_op jit(solution)/shard_map/pallas_call | solution.py:153
  52.8 1.0 copy-done.7
  53.8 5.1 %all-to-all-done.1 = f32[128,1,128]{2,1,0:T(1,128)S(1)} async-done(((f32[128,1,128]{2,1,0:T(1,128)}), f32[128,1,128]{2,1,0:T(1,128)S(1)}, u32[]{:S(2)}, u32[]{:S(2)}) %all-to-all-start.1) | async-done | bytes 65568 | tf_op jit(solution)/shard_map/all_to_all | solution.py:21
  58.8 1.0 copy-done.4
  59.9 1.2 copy-done.6
  61.1 1.2 copy-done.8
  62.3 2.2 %shard_map.88.w_ref = bf16[256,4096]{1,0:T(8,128)(2,1)S(1)} custom-call(s32[2]{0:T(128)S(1)} %pad_add_fusion.here_ref, f32[128,128]{1,0:T(8,128)S(1)} %bitcast.43, f32[64,2048]{1,0:T(8,128)S(1)} %bitcast.37, s32[64,2048]{1,0:T(8,128)S(1)} %bitcast.39, s32[64,2048]{1,0:T(8,128)S(1)} %bitcast.40, f32[128,2048]{1,0:T(8,128)S(1)} %copy-done.6, ...), custom_call_target="tpu_custom_call" | custom-call | tf_op jit(solution)/shard_map/pallas_call | solution.py:165
  64.5 10.5 %shard_map.89 = f32[16,4,64,256]{3,2,1,0:T(8,128)S(1)} custom-call(bf16[256,4096]{1,0:T(8,128)(2,1)S(1)} %shard_map.88.w_ref, f32[128,2048]{1,0:T(8,128)S(1)} %bitcast_convert_fusion.own_ref, f32[128,2048]{1,0:T(8,128)S(1)} %convert_element_type.35.mate_ref), custom_call_target="tpu_custom_call" | custom-call | tf_op jit(solution)/shard_map/pallas_call | solution.py:175
  75.5 27.0 %all_to_all.32 = f16[16,4,64,256]{3,2,1,0:T(8,128)(2,1)S(1)} all-to-all(f16[16,4,64,256]{3,2,1,0:T(8,128)(2,1)S(1)} %convert_element_type.36), channel_id=1, replica_groups=mesh['far'=4,'mate'=2,'across'=4,'down'=4,'feat'=2] {'across','down'}, dimensions={0} | all-to-all | bytes 4194304 | tf_op jit(solution)/shard_map/all_to_all | solution.py:21
  102.9 19.8 %all_to_all.33 = f32[8,32,256]{2,1,0:T(8,128)S(1)} all-to-all(f32[8,32,256]{2,1,0:T(8,128)S(1)} %bitcast.45), channel_id=1, replica_groups=mesh['far'=4,'mate'=2,'across'=4,'down'=4,'feat'=2] {'far','feat'}, dimensions={0} | all-to-all | bytes 524288 | tf_op jit(solution)/shard_map/all_to_all | solution.py:21
  (38 shorter events, 6.4 us)
Async XLA Ops:
  0.6 49.0 %collective-permute-start = (f32[64,2048]{1,0:T(8,128)}, f32[64,2048]{1,0:T(8,128)}, u32[]{:S(2)}, u32[]{:S(2)}) collective-permute-start(f32[64,2048]{1,0:T(8,128)} %bitcast.34), channel_id=1, source_target_pairs={{0,32},{32,0},{1,33},{33,1},{2,34},{34,2},{3,35},{35,3},{4,36},{36... | collective-permute-start | bytes 1572872 | tf_op jit(solution)/shard_map/ppermute | solution.py:136
  3.2 1.1 copy-start
  5.0 26.4 %all-to-all-start = ((f32[128,1,64]{2,1,0:T(1,128)}), f32[128,1,64]{2,1,0:T(1,128)S(1)}, u32[]{:S(2)}, u32[]{:S(2)}) async-start(f32[128,1,64]{2,1,0:T(1,128)} %bitcast.6), calls=%async_computation | async-start | bytes 131072 | tf_op jit(solution)/shard_map/all_to_all | solution.py:21
  21.4 28.2 %collective-permute-start.1 = (bf16[64,2048]{1,0:T(8,128)(2,1)}, bf16[64,2048]{1,0:T(8,128)(2,1)S(1)}, u32[]{:S(2)}, u32[]{:S(2)}) collective-permute-start(bf16[64,2048]{1,0:T(8,128)(2,1)} %bitcast_convert_fusion.2), channel_id=1, source_target_pairs={{0,32},{32,0},{1,33},{33,1},{2,34},{34,2},{3,35},{35,3},{4,36},{36... | collective-permute-start | bytes 786440 | tf_op jit(solution)/shard_map/ppermute | solution.py:136
  25.3 1.0 copy-start.3
  25.3 1.0 copy-start.9
  27.3 31.5 %collective-permute-start.2 = (bf16[64,2048]{1,0:T(8,128)(2,1)}, bf16[64,2048]{1,0:T(8,128)(2,1)}, u32[]{:S(2)}, u32[]{:S(2)}) collective-permute-start(bf16[64,2048]{1,0:T(8,128)(2,1)} %get-tuple-element.31), channel_id=1, source_target_pairs={{0,32},{32,0},{1,33},{33,1},{2,34},{34,2},{3,35},{35,3},{4,36},{36... | collective-permute-start | bytes 786440 | tf_op jit(solution)/shard_map/ppermute | solution.py:136
  28.2 3.2 %copy-start.1 = (f32[2048,64]{0,1:T(8,128)S(1)}, f32[2048,64]{0,1:T(8,128)}, u32[]{:S(2)}) copy-start(f32[2048,64]{0,1:T(8,128)} %param.6) | copy-start | bytes 1572868
  28.2 3.2 %copy-start.2 = (s32[2048,64]{0,1:T(8,128)S(1)}, s32[2048,64]{0,1:T(8,128)}, u32[]{:S(2)}) copy-start(s32[2048,64]{0,1:T(8,128)} %param.7) | copy-start | bytes 1572868
  30.7 17.8 %collective-permute-start.3 = (bf16[128,2048]{1,0:T(8,128)(2,1)S(1)}, bf16[128,2048]{1,0:T(8,128)(2,1)}, u32[]{:S(2)}, u32[]{:S(2)}) collective-permute-start(bf16[128,2048]{1,0:T(8,128)(2,1)S(1)} %bitcast.48), channel_id=1, source_target_pairs={{0,32},{32,0},{1,33},{33,1},{2,34},{34,2},{3,35},{35,3},{4,36},{36... | collective-permute-start | bytes 1572872 | tf_op jit(solution)/shard_map/ppermute | solution.py:136
  34.1 1.0 copy-start.5
  35.0 23.8 %all-to-all-start.1 = ((f32[128,1,128]{2,1,0:T(1,128)}), f32[128,1,128]{2,1,0:T(1,128)S(1)}, u32[]{:S(2)}, u32[]{:S(2)}) async-start(f32[128,1,128]{2,1,0:T(1,128)} %bitcast.9), calls=%async_computation.1 | async-start | bytes 131072 | tf_op jit(solution)/shard_map/all_to_all | solution.py:21
  52.8 1.0 copy-start.7
  58.8 1.0 copy-start.4
  59.9 1.2 copy-start.6
  61.1 1.2 copy-start.8

commit v3 on v2

v3 whole, which is shorter than its diff:
```python
import jax
import jax.numpy as jnp
from jax import lax
from jax.experimental import pallas as pl
from jax.experimental.pallas import tpu as pltpu
from jax.sharding import Mesh
from jax.sharding import PartitionSpec as P


BINS = 32
LEAVES = 2
AXES = ("far", "mate", "across", "down", "feat")
ROWS = AXES[:4]
PLANE = ("across", "down")
BLOCK = 256
F32 = jnp.float32
VMEM = 28 << 20
DOWN = 2.0**-3


def swap(x, axis):
    return lax.all_to_all(x, axis, split_axis=0, concat_axis=0, tiled=True)


def chosen_sum(got, here, earlier):
    index = lax.broadcasted_iota(jnp.int32, got.shape, 0)
    chosen = (index < here) if earlier else (index > here)
    return jnp.sum(jnp.where(chosen, got, 0.0), axis=0, keepdims=True)


def as_column(line):
    n = line.shape[1]
    row = lax.broadcasted_iota(jnp.int32, (n, n), 0)
    col = lax.broadcasted_iota(jnp.int32, (n, n), 1)
    return jnp.sum(jnp.where(row == col, jnp.broadcast_to(line, (n, n)), 0.0), axis=1, keepdims=True)


def as_line(column):
    n = column.shape[0]
    row = lax.broadcasted_iota(jnp.int32, (n, n), 0)
    col = lax.broadcasted_iota(jnp.int32, (n, n), 1)
    return jnp.sum(jnp.where(row == col, jnp.broadcast_to(column, (n, n)), 0.0), axis=0, keepdims=True)


def split_dot(x, ones):
    high = x.astype(jnp.bfloat16)
    rest = x - high.astype(F32)
    middle = rest.astype(jnp.bfloat16)
    low = (rest - middle.astype(F32)).astype(jnp.bfloat16)
    dot = lambda part: lax.dot(part, ones, preferred_element_type=F32)
    return (dot(low) + dot(middle)) + dot(high)


def total_kernel(score_ref, total_ref):
    total = jnp.sum(jnp.exp(score_ref[...]), axis=1, keepdims=True)
    total_ref[...] = jnp.broadcast_to(as_line(total), total_ref.shape)


def hazards(here, score_ref, event_ref, later_ref):
    width, rows = score_ref.shape
    row = lax.broadcasted_iota(jnp.int32, (BLOCK, BLOCK), 0)
    col = lax.broadcasted_iota(jnp.int32, (BLOCK, BLOCK), 1)
    suffix = (row >= col).astype(F32).astype(jnp.bfloat16)
    blocks = rows // BLOCK
    at = lambda k: pl.ds(k * BLOCK, BLOCK)
    e = jnp.concatenate([jnp.exp(score_ref[:, at(k)]) for k in range(blocks)], axis=0)
    runs = split_dot(e, suffix)
    carry = as_column(chosen_sum(later_ref[...], here, False))
    both = [None] * blocks
    for k in reversed(range(blocks)):
        run = runs[k * width : (k + 1) * width]
        inverse = 1.0 / (run + carry)
        carry = carry + run[:, :1]
        share = event_ref[:, at(k)].astype(F32) * inverse
        both[k] = jnp.concatenate([share, share * inverse], axis=0)
    return e, both


def sums_kernel(here_ref, score_ref, event_ref, later_ref, total_ref):
    _, both = hazards(here_ref[0], score_ref, event_ref, later_ref)
    total = jnp.sum(sum(both[1:], both[0]), axis=1, keepdims=True)
    total_ref[...] = jnp.broadcast_to(as_line(total), total_ref.shape)


def local_kernel(here_ref, later_ref, *refs):
    out_ref = refs[-1]
    for part in range(2):
        score_ref, event_ref, leaf_ref = refs[3 * part : 3 * part + 3]
        width, rows = score_ref.shape
        e, both = hazards(here_ref[part], score_ref, event_ref, later_ref)
        row = lax.broadcasted_iota(jnp.int32, (BLOCK, BLOCK), 0)
        col = lax.broadcasted_iota(jnp.int32, (BLOCK, BLOCK), 1)
        prefix = (row <= col).astype(F32).astype(jnp.bfloat16)
        runs = split_dot(jnp.concatenate(both, axis=0), prefix)
        carry = jnp.zeros((2 * width, 1), F32)
        for k in range(rows // BLOCK):
            at = pl.ds(k * BLOCK, BLOCK)
            run = runs[2 * k * width : 2 * (k + 1) * width]
            here = run + carry
            carry = carry + run[:, BLOCK - 1 :]
            x = e[k * width : (k + 1) * width]
            product = x * here[:width]
            out_ref[3 * part, :, at] = product - event_ref[:, at].astype(F32)
            out_ref[3 * part + 1, :, at] = product - x * x * here[width:]
            out_ref[3 * part + 2, :, at] = jnp.where(leaf_ref[:, at].astype(F32) == 0.0, x, -x)


def weigh_kernel(here_ref, base_ref, held, w_ref):
    _, width, rows = held.shape
    for part in range(2):
        base = as_column(chosen_sum(base_ref[...], here_ref[part], True))
        for k in range(rows // BLOCK):
            at = pl.ds(k * BLOCK, BLOCK)
            signed = held[3 * part + 2, :, at]
            e = jnp.abs(signed)
            carried = e * base[:width]
            g = (held[3 * part, :, at] + carried) * DOWN
            h = (held[3 * part + 1, :, at] + (carried - e * e * base[width:])) * DOWN
            for n, v in enumerate((g, h)):
                for m in range(LEAVES):
                    keep = (signed < 0.0) if m else (signed > 0.0)
                    w_ref[
                        pl.ds((n * LEAVES + m) * width, width), pl.ds(part * rows + k * BLOCK, BLOCK)
                    ] = jnp.where(keep, v, 0.0).astype(jnp.bfloat16)


def hist_kernel(w_ref, own_ref, mate_ref, out_ref, line_ref):
    feats, rows = own_ref.shape
    line_ref[:, :rows] = own_ref[...].astype(F32)
    line_ref[:, rows:] = mate_ref[...].astype(F32)
    level = lax.broadcasted_iota(jnp.int32, (BINS, 2 * rows), 0).astype(F32).astype(jnp.bfloat16)
    one = jnp.ones((), jnp.bfloat16)
    zero = jnp.zeros((), jnp.bfloat16)
    tiles = []
    for i in range(feats):
        line = jnp.broadcast_to(line_ref[pl.ds(i, 1), :], (BINS, 2 * rows)).astype(jnp.bfloat16)
        tiles.append(jnp.where(line == level, one, zero))
    hot = jnp.concatenate(tiles, axis=0)
    got = lax.dot_general(hot, w_ref[...], (((1,), (1,)), ((), ())), preferred_element_type=F32)
    out_ref[:, 0] = got.reshape(out_ref.shape[0], *out_ref.shape[2:])


def per_device(score, event, leaf, bins, split_feature, split_bin):
    rows, width = score.shape
    shards = lax.axis_size(ROWS)
    cores = lax.axis_size("feat")
    cols = 2 * LEAVES * width
    far, mate, across, down = (lax.axis_size(a) for a in ROWS)
    members = across * down
    here = lax.axis_index(ROWS).astype(jnp.int32)
    both = jnp.stack([here, here ^ members])
    scalar = pl.BlockSpec(memory_space=pltpu.SMEM)
    dense = pl.BlockSpec(memory_space=pltpu.VMEM)
    limit = pltpu.CompilerParams(vmem_limit_bytes=VMEM)
    pair = [(0, 1), (1, 0)]
    send = lambda x: lax.ppermute(x, "mate", pair)
    mate_score = send(score.T)
    copies = pl.pallas_call(
        total_kernel,
        out_shape=jax.ShapeDtypeStruct((shards, width), F32),
        compiler_params=limit,
    )(score.T)
    copies, score, event, leaf, bins = lax.optimization_barrier((copies, score, event, leaf, bins))
    totals = swap(copies, ROWS)
    columns = bins.T.astype(jnp.bfloat16).reshape(far, mate, -1, rows)
    side = lax.axis_index("mate")
    pick = lambda k: lax.dynamic_index_in_dim(columns, k, 1, keepdims=False).reshape(-1, rows)
    own_columns = pick(side)
    mate_event = send(event.T.astype(jnp.bfloat16))
    mate_columns = send(pick(1 - side))
    mate_leaf = send(leaf.T.astype(jnp.bfloat16))

    copies = pl.pallas_call(
        sums_kernel,
        in_specs=[scalar, dense, dense, dense],
        out_shape=jax.ShapeDtypeStruct((shards, 2 * width), F32),
        compiler_params=limit,
    )(both, score.T, event.T, totals)
    copies, split_feature, routed = lax.optimization_barrier((copies, split_feature, leaf))
    base = swap(copies, ROWS)
    split_value = jnp.take(bins, split_feature, axis=1)
    new_leaf = 2 * routed + (split_value > split_bin[None, :]).astype(jnp.int32)
    base, new_leaf = lax.optimization_barrier((base, new_leaf))
    locals_ = pl.pallas_call(
        local_kernel,
        in_specs=[scalar] + [dense] * 7,
        out_shape=jax.ShapeDtypeStruct((6, width, rows), F32),
    )(both, totals, score.T, event.T, leaf.T, mate_score, mate_event, mate_leaf)
    weights = pl.pallas_call(
        weigh_kernel,
        in_specs=[scalar, dense, dense],
        out_shape=jax.ShapeDtypeStruct((cols, 2 * rows), jnp.bfloat16),
        compiler_params=limit,
    )(both, base, locals_)
    own = cores * BINS
    step = members // 2
    slab = step * cores
    columns = pl.BlockSpec((slab, rows), lambda z, j: (2 * z + j, 0))
    parts = pl.pallas_call(
        hist_kernel,
        grid=(far, 2),
        in_specs=[pl.BlockSpec((cols, 2 * rows), lambda z, j: (0, 0)), columns, columns],
        out_specs=pl.BlockSpec((step, 1, own, cols), lambda z, j: (j, z, 0, 0)),
        out_shape=jax.ShapeDtypeStruct((members, far, own, cols), F32),
        scratch_shapes=[pltpu.VMEM((slab, 2 * rows), F32)],
        compiler_params=limit,
    )(weights, own_columns, mate_columns)
    got = jnp.sum(swap(parts.astype(jnp.float16), PLANE).astype(F32), axis=0)
    got = swap(got.reshape(far * cores, BINS, cols), ("far", "feat"))
    summed = jnp.sum(got.reshape(far, cores, BINS, cols), axis=0)
    summed = summed * (BINS * LEAVES / (rows * shards) / DOWN)
    summed = summed.reshape(cores, BINS, 2, LEAVES, width)
    summed = jnp.moveaxis(summed, 0, 3).reshape(1, BINS, 2, LEAVES, cores * width)
    return (summed[:, :, 0], summed[:, :, 1], new_leaf)


def solution(mesh):
    finer = Mesh(
        mesh.devices.reshape(4, 2, 4, 4, mesh.shape["feat"]), AXES
    )
    in_specs = (
        P(ROWS, "feat"),
        P(ROWS, "feat"),
        P(ROWS, "feat"),
        P(ROWS, None),
        P("feat"),
        P("feat"),
    )
    out_specs = (P(AXES, None, None, None), P(AXES, None, None, None), P(ROWS, "feat"))
    return jax.shard_map(per_device, mesh=finer, in_specs=in_specs, out_specs=out_specs, check_vma=False)
```

time: 125 us -> 123 us (0.984)
  waiting for transfers between devices: 5.08 us -> 7.38 us
  blocking collectives: 46.8 us -> 44.8 us
  local copies, waits for them, and re-layouts: 12.5 us -> 10.7 us
    unnamed x22 -> x26, local copies, waits for them, and re-layouts: 8.11 us -> 4.98 us
    all_to_all x2, waiting for transfers between devices: 5.07 us -> 7.37 us  [swap(): return lax.all_to_all(x, axis, split_axis=0, concat_axis=0, tiled=True)]
    all_to_all x2, blocking collectives: 46.8 us -> 44.8 us  [swap(): return lax.all_to_all(x, axis, split_axis=0, concat_axis=0, tiled=True)]
    gather x1, local copies, waits for them, and re-layouts: 0.76 us -> 2.64 us  [per_device(): split_value = jnp.take(bins, split_feature, axis=1)]
  transfers between devices with their start and end apart: 6 -> 6, of which waited for: 1 -> 2; matrix products, arithmetic and copies ran while one was open for 9% -> 10% of each run, Pallas kernels for 5% -> 8%
where the time goes in v3:
time: 123 us
  blocking collectives  44.8 us (36%)
  starting transfers between devices  32 us (26%)
  Pallas kernels  19.9 us (16%)
  local copies, waits for them, and re-layouts  10.7 us (9%)
  waiting for transfers between devices  7.38 us (6%)
  other arithmetic  7.37 us (6%)
    all_to_all x2, blocking collectives, swap(): return lax.all_to_all(x, axis, split_axis=0, concat_axis=0, tiled=True)  44.8 us
    all_to_all x2, starting transfers between devices, swap(): return lax.all_to_all(x, axis, split_axis=0, concat_axis=0, tiled=True)  27.4 us
    pallas_call x1, Pallas kernels, per_device(): pl.pallas_call(hist_kernel, grid=(far, 2), in_specs=[pl.BlockSpec((cols,...  10.6 us
    all_to_all x2, waiting for transfers between devices, swap(): return lax.all_to_all(x, axis, split_axis=0, concat_axis=0, tiled=True)  7.37 us
    pallas_call x1, Pallas kernels, per_device(): pl.pallas_call(local_kernel, in_specs=[scalar] + [dense] * 7, out_shape=j...  5.29 us
    unnamed x26, local copies, waits for them, and re-layouts  4.98 us
    ppermute x4, starting transfers between devices, per_device(): send = lambda x: lax.ppermute(x, 'mate', pair)  4.59 us
    gather x1, local copies, waits for them, and re-layouts, per_device(): split_value = jnp.take(bins, split_feature, axis=1)  2.64 us
  transfers between devices with their start and end apart: 6, of which 2 were waited for; matrix products, arithmetic and copies ran while one was open for 10% of the time, Pallas kernels for 8%

profile of v3, /device:TPU:1, one launch (start us, length us, event | category | flops | bytes accessed | tf_op | source)
XLA Modules:
  0.0 123.0 jit_solution(3690257198961760312)
XLA Ops:
  0.6 2.5 %collective-permute-start = (f32[64,2048]{1,0:T(8,128)}, f32[64,2048]{1,0:T(8,128)}, u32[]{:S(2)}, u32[]{:S(2)}) collective-permute-start(f32[64,2048]{1,0:T(8,128)} %bitcast.32), channel_id=1, source_target_pairs={{0,32},{32,0},{1,33},{33,1},{2,34},{34,2},{3,35},{35,3},{4,36},{36... | collective-permute-start | bytes 1572872 | tf_op jit(solution)/shard_map/ppermute | solution.py:156
  3.2 1.1 copy-done.1
  4.2 0.8 shard_map.85
  5.0 14.6 %all-to-all-start = ((f32[128,1,64]{2,1,0:T(1,128)}), f32[128,1,64]{2,1,0:T(1,128)S(1)}, u32[]{:S(2)}, u32[]{:S(2)}) async-start(f32[128,1,64]{2,1,0:T(1,128)} %bitcast.6), calls=%async_computation | async-start | bytes 131072 | tf_op jit(solution)/shard_map/all_to_all | solution.py:22
  19.7 1.8 %bitcast_convert_fusion = bf16[64,2048]{1,0:T(8,128)(2,1)} fusion(s32[2048,64]{0,1:T(8,128)} %param.8), kind=kLoop, calls=%fused_computation.13 | loop fusion | flops 131072 | bytes 786432 | tf_op jit(solution)/shard_map/convert_element_type | solution.py:171
  22.0 1.8 %bitcast_convert_fusion.1 = bf16[64,2048]{1,0:T(8,128)(2,1)} fusion(s32[2048,64]{0,1:T(8,128)} %param.7), kind=kLoop, calls=%fused_computation.14 | loop fusion | flops 131072 | bytes 786432 | tf_op jit(solution)/shard_map/convert_element_type | solution.py:169
  23.8 0.9 collective-permute-start.1
  24.7 1.8 %copy.28 = s32[2048,256]{0,1:T(8,128)} copy(s32[2048,256]{1,0:T(8,128)S(1)} %copy-done.8) | data formatting | bytes 4194304 | tf_op jit(solution)/shard_map/optimization_barrier | solution.py:163
  26.5 1.8 %convert_element_type.24 = bf16[2048,256]{0,1:T(8,128)(2,1)S(1)} convert(s32[2048,256]{0,1:T(8,128)} %copy.28) | non-fusion elementwise | flops 524288 | bytes 3145728 | tf_op jit(solution)/shard_map/convert_element_type | solution.py:165
  28.4 0.9 constant_dynamic-slice_fusion
  30.4 1.8 %shard_map.86 = f32[128,128]{1,0:T(8,128)} custom-call(s32[2]{0:T(128)S(1)} %pad_add_fusion.here_ref, f32[64,2048]{1,0:T(8,128)S(1)} %bitcast.35, s32[64,2048]{1,0:T(8,128)S(1)} %bitcast.37, f32[128,64]{1,0:T(8,128)S(1)} %bitcast.39), custom_call_target="tpu_custom_call" | custom-call | tf_op jit(solution)/shard_map/pallas_call | solution.py:173
  32.2 12.8 %all-to-all-start.1 = ((f32[128,1,128]{2,1,0:T(1,128)}), f32[128,1,128]{2,1,0:T(1,128)S(1)}, u32[]{:S(2)}, u32[]{:S(2)}) async-start(f32[128,1,128]{2,1,0:T(1,128)} %bitcast.9), calls=%async_computation.1 | async-start | bytes 131072 | tf_op jit(solution)/shard_map/all_to_all | solution.py:22
  45.1 2.6 %gather_fusion = s32[64,2048]{1,0:T(8,128)S(1)} fusion(s32[2048,256]{0,1:T(8,128)} %copy.28, s32[1024]{0:T(1024)S(1)} %pad_clamp_fusion), kind=kCustom, calls=%fused_computation | custom fusion | bytes 1048832 | tf_op jit(solution)/shard_map/jit(_take)/gather | solution.py:181
  47.7 1.0 bitcast_add_fusion
  48.8 7.0 %all-to-all-done.1 = f32[128,1,128]{2,1,0:T(1,128)S(1)} async-done(((f32[128,1,128]{2,1,0:T(1,128)}), f32[128,1,128]{2,1,0:T(1,128)S(1)}, u32[]{:S(2)}, u32[]{:S(2)}) %all-to-all-start.1) | async-done | bytes 65568 | tf_op jit(solution)/shard_map/all_to_all | solution.py:22
  55.8 0.7 copy-done.9
  56.4 5.3 %shard_map.87.held = f32[6,64,2048]{2,1,0:T(8,128)} custom-call(s32[2]{0:T(128)} %copy-done.5, f32[128,64]{1,0:T(8,128)} %bitcast.40, f32[64,2048]{1,0:T(8,128)} %bitcast.33, s32[64,2048]{1,0:T(8,128)} %bitcast.36, s32[64,2048]{1,0:T(8,128)} %bitcast.42, f32[64,2048]{1,0:T(8,128)} %collective-permute-done.refs_3_, ...), custom_call_target="tpu_custom_call" | custom-call | tf_op jit(solution)/shard_map/pallas_call | solution.py:184
  61.7 1.9 %copy-done = f32[6,64,2048]{2,1,0:T(8,128)S(1)} copy-done((f32[6,64,2048]{2,1,0:T(8,128)S(1)}, f32[6,64,2048]{2,1,0:T(8,128)}, u32[]{:S(2)}) %copy-start) | copy-done | bytes 3145752
  63.6 1.4 %shard_map.88.w_ref = bf16[256,4096]{1,0:T(8,128)(2,1)S(1)} custom-call(s32[2]{0:T(128)S(1)} %copy-done.6, f32[128,128]{1,0:T(8,128)S(1)} %bitcast.41, f32[6,64,2048]{2,1,0:T(8,128)S(1)} %copy-done), custom_call_target="tpu_custom_call" | custom-call | tf_op jit(solution)/shard_map/pallas_call | solution.py:189
  65.0 10.6 %shard_map.89 = f32[16,4,64,256]{3,2,1,0:T(8,128)S(1)} custom-call(bf16[256,4096]{1,0:T(8,128)(2,1)S(1)} %shard_map.88.w_ref, bf16[128,2048]{1,0:T(8,128)(2,1)S(1)} %bitcast.38, bf16[128,2048]{1,0:T(8,128)(2,1)S(1)} %collective-permute-done.3.mate_ref), custom_call_target="tpu_custom_call" | custom-call | tf_op jit(solution)/shard_map/pallas_call | solution.py:199
  76.1 27.2 %all_to_all.33 = f16[16,4,64,256]{3,2,1,0:T(8,128)(2,1)S(1)} all-to-all(f16[16,4,64,256]{3,2,1,0:T(8,128)(2,1)S(1)} %convert_element_type.26), channel_id=1, replica_groups=mesh['far'=4,'mate'=2,'across'=4,'down'=4,'feat'=2] {'across','down'}, dimensions={0} | all-to-all | bytes 4194304 | tf_op jit(solution)/shard_map/all_to_all | solution.py:22
  103.7 17.6 %all_to_all.34 = f32[8,32,256]{2,1,0:T(8,128)S(1)} all-to-all(f32[8,32,256]{2,1,0:T(8,128)S(1)} %bitcast.44), channel_id=1, replica_groups=mesh['far'=4,'mate'=2,'across'=4,'down'=4,'feat'=2] {'far','feat'}, dimensions={0} | all-to-all | bytes 524288 | tf_op jit(solution)/shard_map/all_to_all | solution.py:22
  121.7 0.6 copy.32
  122.3 0.6 copy.31
  (40 shorter events, 2.9 us)
Async XLA Ops:
  0.6 55.1 %collective-permute-start = (f32[64,2048]{1,0:T(8,128)}, f32[64,2048]{1,0:T(8,128)}, u32[]{:S(2)}, u32[]{:S(2)}) collective-permute-start(f32[64,2048]{1,0:T(8,128)} %bitcast.32), channel_id=1, source_target_pairs={{0,32},{32,0},{1,33},{33,1},{2,34},{34,2},{3,35},{35,3},{4,36},{36... | collective-permute-start | bytes 1572872 | tf_op jit(solution)/shard_map/ppermute | solution.py:156
  3.2 1.1 copy-start.1
  4.2 20.5 %copy-start.8 = (s32[2048,256]{1,0:T(8,128)S(1)}, s32[2048,256]{1,0:T(8,128)}, u32[]{:S(2)}) copy-start(s32[2048,256]{1,0:T(8,128)} %param.9) | copy-start | bytes 6291460
  5.0 25.3 %all-to-all-start = ((f32[128,1,64]{2,1,0:T(1,128)}), f32[128,1,64]{2,1,0:T(1,128)S(1)}, u32[]{:S(2)}, u32[]{:S(2)}) async-start(f32[128,1,64]{2,1,0:T(1,128)} %bitcast.6), calls=%async_computation | async-start | bytes 131072 | tf_op jit(solution)/shard_map/all_to_all | solution.py:22
  21.4 34.3 %collective-permute-start.2 = (bf16[64,2048]{1,0:T(8,128)(2,1)}, bf16[64,2048]{1,0:T(8,128)(2,1)S(1)}, u32[]{:S(2)}, u32[]{:S(2)}) collective-permute-start(bf16[64,2048]{1,0:T(8,128)(2,1)} %bitcast_convert_fusion), channel_id=1, source_target_pairs={{0,32},{32,0},{1,33},{33,1},{2,34},{34,2},{3,35},{35,3},{4,36},{36... | collective-permute-start | bytes 786440 | tf_op jit(solution)/shard_map/ppermute | solution.py:156
  23.8 31.9 %collective-permute-start.1 = (bf16[64,2048]{1,0:T(8,128)(2,1)}, bf16[64,2048]{1,0:T(8,128)(2,1)}, u32[]{:S(2)}, u32[]{:S(2)}) collective-permute-start(bf16[64,2048]{1,0:T(8,128)(2,1)} %bitcast_convert_fusion.1), channel_id=1, source_target_pairs={{0,32},{32,0},{1,33},{33,1},{2,34},{34,2},{3,35},{35,3},{4,36},{36... | collective-permute-start | bytes 786440 | tf_op jit(solution)/shard_map/ppermute | solution.py:156
  26.5 3.8 %copy-start.2 = (f32[2048,64]{0,1:T(8,128)S(1)}, f32[2048,64]{0,1:T(8,128)}, u32[]{:S(2)}) copy-start(f32[2048,64]{0,1:T(8,128)} %param.6) | copy-start | bytes 1572868
  26.5 3.8 %copy-start.3 = (s32[2048,64]{0,1:T(8,128)S(1)}, s32[2048,64]{0,1:T(8,128)}, u32[]{:S(2)}) copy-start(s32[2048,64]{0,1:T(8,128)} %param.7) | copy-start | bytes 1572868
  28.4 3.8 %copy-start.11 = (s32[64]{0:T(128)S(1)}, s32[64]{0:T(128)}, u32[]{:S(2)}) copy-start(s32[64]{0:T(128)} %param.10) | copy-start | bytes 772
  29.3 35.7 %collective-permute-start.3 = (bf16[128,2048]{1,0:T(8,128)(2,1)}, bf16[128,2048]{1,0:T(8,128)(2,1)S(1)}, u32[]{:S(2)}, u32[]{:S(2)}) collective-permute-start(bf16[128,2048]{1,0:T(8,128)(2,1)} %bitcast.17), channel_id=1, source_target_pairs={{0,32},{32,0},{1,33},{33,1},{2,34},{34,2},{3,35},{35,3},{4,36},{36... | collective-permute-start | bytes 1572872 | tf_op jit(solution)/shard_map/ppermute | solution.py:156
  30.0 17.7 %copy-start.5 = (s32[2]{0:T(128)}, s32[2]{0:T(128)S(1)}, u32[]{:S(2)}) copy-start(s32[2]{0:T(128)S(1)} %pad_add_fusion.here_ref) | copy-start | bytes 28
  30.4 17.4 %copy-start.4 = (f32[128,1,64]{2,1,0:T(1,128)}, f32[128,1,64]{2,1,0:T(1,128)S(1)}, u32[]{:S(2)}) copy-start(f32[128,1,64]{2,1,0:T(1,128)S(1)} %all-to-all-done) | copy-start | bytes 98308
  32.2 23.5 %all-to-all-start.1 = ((f32[128,1,128]{2,1,0:T(1,128)}), f32[128,1,128]{2,1,0:T(1,128)S(1)}, u32[]{:S(2)}, u32[]{:S(2)}) async-start(f32[128,1,128]{2,1,0:T(1,128)} %bitcast.9), calls=%async_computation.1 | async-start | bytes 131072 | tf_op jit(solution)/shard_map/all_to_all | solution.py:22
  45.0 2.7 %copy-start.7 = (s32[2048,64]{0,1:T(8,128)S(1)}, s32[2048,64]{0,1:T(8,128)}, u32[]{:S(2)}) copy-start(s32[2048,64]{0,1:T(8,128)} %param.8) | copy-start | bytes 1572868
  45.0 2.7 %copy-start.10 = (s32[64]{0:T(128)S(1)}, s32[64]{0:T(128)}, u32[]{:S(2)}) copy-start(s32[64]{0:T(128)} %param.11) | copy-start | bytes 772
  55.7 0.7 copy-start.9
  56.4 5.3 %copy-start.6 = (s32[2]{0:T(128)S(1)}, s32[2]{0:T(128)}, u32[]{:S(2)}) copy-start(s32[2]{0:T(128)} %copy-done.5) | copy-start | bytes 28
  61.7 1.9 %copy-start = (f32[6,64,2048]{2,1,0:T(8,128)S(1)}, f32[6,64,2048]{2,1,0:T(8,128)}, u32[]{:S(2)}) copy-start(f32[6,64,2048]{2,1,0:T(8,128)} %shard_map.87.held) | copy-start | bytes 9437188
